TPU v7x, 8 devices: a whole 2x2x1 slice. The times are simulated.
8 devices in a mesh: dp: 2 (over y, z), tp: 4 (over x, core).
Axes of the slice: x: 2, y: 2, z: 1, core: 2. Of those that a mesh axis runs over, the one named last changes fastest.
Arguments:
- x: bfloat16 [4096, 1024], P('dp'), parts along dimension 0
- dy: bfloat16 [4096, 1024], P('dp'), parts along dimension 0
- gate: bfloat16 [4096, 3072], P('dp', 'tp'), parts along dimension 0
- up: bfloat16 [4096, 3072], P('dp', 'tp'), parts along dimension 0
- w_gate: bfloat16 [1024, 3072], P(None, 'tp')
- w_up: bfloat16 [1024, 3072], P(None, 'tp')
- w_down: bfloat16 [3072, 1024], P('tp')
Outputs:
- output 1: bfloat16 [4096, 1024], P('dp'), parts along dimension 0
- output 2: bfloat16 [2048, 3072], P('dp', 'tp'), parts along dimension 0
- output 3: bfloat16 [2048, 3072], P('dp', 'tp'), parts along dimension 0
- output 4: bfloat16 [6144, 1024], P(('dp', 'tp')), parts along dimension 0
There are 2 independent parts. A program takes and returns all parts, laid end to end along the dimension named above; an argument that names none is the same for every part.
All inputs are finite; a program needn't handle non-finite values.
Results may differ from a plain program's by a relative error of at most 0.012.
Values are sent between devices in bfloat16 or wider.
A program may use at most 2 GiB of HBM per device.

v0:
```python
import jax
import jax.numpy as jnp
from jax import lax
from jax.sharding import PartitionSpec as P


def act(gate, up):
    return jax.nn.silu(gate) * up


def solution(mesh):
    def step(x, dy, gate, up, w_gate, w_up, w_down):
        hidden, back = jax.vjp(act, gate.astype(jnp.float32), up.astype(jnp.float32))
        d_hidden = jnp.dot(dy, w_down.T, preferred_element_type=jnp.float32)
        d_gate, d_up = (g.astype(jnp.bfloat16) for g in back(d_hidden))
        term = jnp.dot(d_gate, w_gate.T, preferred_element_type=jnp.float32) + jnp.dot(d_up, w_up.T, preferred_element_type=jnp.float32)
        dx = lax.psum(term.astype(jnp.bfloat16), "tp")
        dw_gate = jnp.dot(x.T, d_gate, preferred_element_type=jnp.float32)
        dw_up = jnp.dot(x.T, d_up, preferred_element_type=jnp.float32)
        dw_down = jnp.dot(hidden.astype(jnp.bfloat16).T, dy, preferred_element_type=jnp.float32)
        return dx, *(g.astype(jnp.bfloat16) for g in (dw_gate, dw_up, dw_down))

    tokens, columns, rows = P("dp", None), P(None, "tp"), P("tp", None)
    return jax.shard_map(
        step,
        mesh=mesh,
        in_specs=(tokens, tokens, P("dp", "tp"), P("dp", "tp"), columns, columns, rows),
        out_specs=(tokens, P("dp", "tp"), P("dp", "tp"), P(("dp", "tp"), None)),
        check_vma=False,
    )
```

profile of v0, /device:TPU:0, one launch (start us, length us, event | category | flops | bytes accessed | tf_op | source)
XLA Modules:
  0.0 121.8 jit_solution(8070193787307195194)
XLA Ops:
  7.2 0.0 copy-start
  7.2 0.0 copy-start.1
  7.2 0.0 all-reduce.2.cloned.1.call-start
  7.2 1.3 %copy-done = bf16[768,1024]{1,0:T(8,128)(2,1)S(1)} copy-done((bf16[768,1024]{1,0:T(8,128)(2,1)S(1)}, bf16[768,1024]{1,0:T(8,128)(2,1)}, u32[]{:S(2)}) %copy-start) | copy-done | bytes 1572888
  8.6 10.4 %multiply_convert_fusion = (bf16[2048,768]{1,0:T(8,128)(2,1)S(1)}, bf16[2048,768]{1,0:T(8,128)(2,1)S(1)}) fusion(bf16[2048,768]{1,0:T(8,128)(2,1)} %param.9, bf16[2048,768]{1,0:T(8,128)(2,1)} %param.10, bf16[2048,1024]{1,0:T(8,128)(2,1)} %param.8, bf16[768,1024]{1,0:T(8,128)(2,1)S(1)} %copy-done), kind=kOutput, calls=%fused_computation.14 | convolution fusion | flops 3246391296 | bytes 18350080 | tf_op jit(solution)/shard_map/dot_general | solution.py:14
  19.0 0.0 copy-start.4
  19.0 0.0 copy-start.3
  19.0 0.0 copy-done.1
  19.0 0.0 copy-start.2
  19.1 3.5 %fusion.15 = f32[2048,1024]{1,0:T(8,128)S(1)} fusion(bf16[2048,768]{1,0:T(8,128)(2,1)S(1)} %get-tuple-element.9, bf16[1024,768]{1,0:T(8,128)(2,1)S(1)} %copy-done.1), kind=kOutput, calls=%fused_computation.22 | convolution fusion | flops 3221225472 | bytes 13107200 | tf_op jit(solution)/shard_map/dot_general | solution.py:16
  22.5 0.0 copy-done.4
  22.5 0.0 copy-done.3
  22.5 0.0 copy-done.2
  22.6 5.0 %add_convert_fusion = bf16[2048,1024]{1,0:T(8,128)(2,1)} fusion(f32[2048,1024]{1,0:T(8,128)S(1)} %fusion.15, bf16[2048,768]{1,0:T(8,128)(2,1)S(1)} %get-tuple-element.8, bf16[1024,768]{1,0:T(8,128)(2,1)S(1)} %copy-done.2), kind=kOutput, calls=%fused_computation.4 | convolution fusion | flops 3225419776 | bytes 17301504 | tf_op jit(solution)/shard_map/dot_general | solution.py:16
  27.6 0.0 all-reduce.2.cloned.1.call-update
  27.6 6.6 %fusion.12 = bf16[1024,768]{0,1:T(8,128)(2,1)S(1)} fusion(bf16[2048,768]{1,0:T(8,128)(2,1)} %copy-done.4, bf16[2048,1024]{1,0:T(8,128)(2,1)} %param.7), kind=kOutput, calls=%fused_computation.19 | convolution fusion | flops 3222011904 | bytes 8912896 | tf_op jit(solution)/shard_map/dot_general | solution.py:18
  34.2 1.6 %copy.11 = bf16[1024,768]{1,0:T(8,128)(2,1)} copy(bf16[1024,768]{0,1:T(8,128)(2,1)S(1)} %fusion.12) | data formatting | bytes 3145728
  35.8 6.6 %fusion.13 = bf16[1024,768]{0,1:T(8,128)(2,1)S(1)} fusion(bf16[2048,768]{1,0:T(8,128)(2,1)} %copy-done.3, bf16[2048,1024]{1,0:T(8,128)(2,1)} %param.7), kind=kOutput, calls=%fused_computation.20 | convolution fusion | flops 3222011904 | bytes 8912896 | tf_op jit(solution)/shard_map/dot_general | solution.py:19
  42.4 1.6 %copy.12 = bf16[1024,768]{1,0:T(8,128)(2,1)} copy(bf16[1024,768]{0,1:T(8,128)(2,1)S(1)} %fusion.13) | data formatting | bytes 3145728
  44.0 9.1 %fusion.9 = bf16[768,1024]{1,0:T(8,128)(2,1)} fusion(bf16[2048,1024]{1,0:T(8,128)(2,1)} %param.8, bf16[2048,768]{1,0:T(8,128)(2,1)} %param.10, bf16[2048,768]{1,0:T(8,128)(2,1)} %param.9), kind=kOutput, calls=%fused_computation.16 | convolution fusion | flops 3234594816 | bytes 12058624 | tf_op jit(solution)/shard_map/dot_general | solution.py:20
  53.1 57.2 %all-reduce.2.cloned.1.call-done = bf16[2048,1024]{1,0:T(8,128)(2,1)} async-done(((bf16[2048,1024]{1,0:T(8,128)(2,1)}), bf16[2048,1024]{1,0:T(8,128)(2,1)}) %all-reduce.2.cloned.1.call-update) | async-done | bytes 4194320 | tf_op jit(solution)/shard_map/psum | solution.py:17
  110.3 4.6 %copy.14 = bf16[2048,1024]{1,0:T(8,128)(2,1)} copy(bf16[2048,1024]{1,0:T(8,128)(2,1)} %all-reduce.2.cloned.1.call-done) | data formatting | bytes 8388608
Async XLA Ops:
  7.2 1.4 %copy-start = (bf16[768,1024]{1,0:T(8,128)(2,1)S(1)}, bf16[768,1024]{1,0:T(8,128)(2,1)}, u32[]{:S(2)}) copy-start(bf16[768,1024]{1,0:T(8,128)(2,1)} %param.13) | copy-start | bytes 4718596
  7.2 11.8 %copy-start.1 = (bf16[1024,768]{1,0:T(8,128)(2,1)S(1)}, bf16[1024,768]{1,0:T(8,128)(2,1)}, u32[]{:S(2)}) copy-start(bf16[1024,768]{1,0:T(8,128)(2,1)} %param.11) | copy-start | bytes 4718596
  7.2 103.1 %all-reduce.2.cloned.1.call-start = ((), (), s32[]{:S(2)}) async-start(), calls=%async_computation | async-start | bytes 8388608 | tf_op jit(solution)/shard_map/psum | solution.py:17
  19.0 3.5 %copy-start.4 = (bf16[2048,768]{1,0:T(8,128)(2,1)}, bf16[2048,768]{1,0:T(8,128)(2,1)S(1)}, u32[]{:S(2)}) copy-start(bf16[2048,768]{1,0:T(8,128)(2,1)S(1)} %get-tuple-element.9) | copy-start | bytes 9437188
  19.0 3.5 %copy-start.3 = (bf16[2048,768]{1,0:T(8,128)(2,1)}, bf16[2048,768]{1,0:T(8,128)(2,1)S(1)}, u32[]{:S(2)}) copy-start(bf16[2048,768]{1,0:T(8,128)(2,1)S(1)} %get-tuple-element.8) | copy-start | bytes 9437188
  19.0 3.5 %copy-start.2 = (bf16[1024,768]{1,0:T(8,128)(2,1)S(1)}, bf16[1024,768]{1,0:T(8,128)(2,1)}, u32[]{:S(2)}) copy-start(bf16[1024,768]{1,0:T(8,128)(2,1)} %param.12) | copy-start | bytes 4718596
Sparse Core Ops, SparseCore 0:
  27.7 82.5 all-reduce.1
where the time goes:
time: 122 us
  waiting for transfers between devices  57.2 us (47%)
  matrix products  41.3 us (34%)
  between operations  14.1 us (12%)
  local copies, waits for them, and re-layouts  9.15 us (8%)
    psum x1, waiting for transfers between devices, step(): dx = lax.psum(term.astype(jnp.bfloat16), 'tp')  57.2 us
    dot_general x1, matrix products, step(): d_hidden = jnp.dot(dy, w_down.T, preferred_element_type=jnp.float32)  10.4 us
    unnamed x13, local copies, waits for them, and re-layouts  9.15 us
    dot_general x1, matrix products, step(): jnp.dot(hidden.astype(jnp.bfloat16).T, dy, preferred_element_type=jnp.flo...  9.14 us
    dot_general x1, matrix products, step(): dw_gate = jnp.dot(x.T, d_gate, preferred_element_type=jnp.float32)  6.61 us
    dot_general x1, matrix products, step(): dw_up = jnp.dot(x.T, d_up, preferred_element_type=jnp.float32)  6.6 us
    dot_general x1, matrix products, step(): jnp.dot(d_up, w_up.T, preferred_element_type=jnp.float32)  5.02 us
    dot_general x1, matrix products, step(): jnp.dot(d_gate, w_gate.T, preferred_element_type=jnp.float32)  3.46 us
  transfers between devices with their start and end apart: 1, of which 1 were waited for; matrix products, arithmetic and copies ran while one was open for 21% of the time, Pallas kernels for 0%

commit v1 on v0

v1 whole, which is shorter than its diff:
```python
import jax
import jax.numpy as jnp
from jax import lax
from jax.experimental import pallas as pl
from jax.experimental.pallas import tpu as pltpu
from jax.sharding import PartitionSpec as P

MESH = pl.DeviceIdType.MESH
F32, BF16 = jnp.float32, jnp.bfloat16
R = 64


def dot_t(a, b):
    return lax.dot_general(a, b, (((1,), (1,)), ((), ())), preferred_element_type=F32)


def dot(a, b):
    return lax.dot_general(a, b, (((1,), (0,)), ((), ())), preferred_element_type=F32)


def kernel(
    x_h, dy_h, gate_h, up_h, wg_h, wu_h, wd_h,
    dx, dwg, dwu, dwd,
    xv, dyv, gv, uv, wgu, wd, dgu, hid, xt, own, tsend, trecv, psend, precv,
    load_sem, blk_sem, t_s, t_r, p_s, p_r, f_s, f_r, o_s, o_r, w_s, w_r,
):
    rows, d = dyv.shape
    f = wd.shape[0]
    half = rows // 2
    steps = rows // (2 * R)
    hs = steps // 2
    me = lax.axis_index("tp")
    chip, core = me // 2, me % 2
    partner, peer = chip * 2 + (1 - core), (1 - chip) * 2 + core

    def base(i):
        return pl.multiple_of(lax.rem((1 - chip) * half + i * (2 * R), rows), 2 * R)

    def block(b, k):
        return pl.ds(pl.multiple_of(b + k * R, R), R)

    def load(i):
        r = pl.ds(base(i), 2 * R)
        return [
            pltpu.make_async_copy(src.at[r], dst.at[r], blk_sem.at[i, n])
            for n, (src, dst) in enumerate(((dy_h, dyv), (gate_h, gv), (up_h, uv)))
        ]

    def remote(src, dst, s, r, i, to):
        return pltpu.make_async_remote_copy(
            src_ref=src, dst_ref=dst, send_sem=s.at[i], recv_sem=r.at[i], device_id={"tp": to}, device_id_type=MESH
        )

    def term_copy(i):
        return remote(tsend.at[i], trecv.at[i], t_s, t_r, i, partner)

    def part_copy(i):
        return remote(psend.at[i], precv.at[i], p_s, p_r, i, peer)

    def mine(j):
        return block(base(hs + j), core)

    def theirs(j):
        return block(base(j), core)

    def final_copy(j):
        r = mine(j)
        return remote(dx.at[r], dx.at[r], f_s, f_r, j, peer)

    def own_copy(j):
        r = mine(j)
        return remote(dx.at[r], dx.at[r], o_s, o_r, j, partner)

    def pass_copy(j):
        r = theirs(j)
        return remote(dx.at[r], dx.at[r], w_s, w_r, j, partner)

    wd_copy = pltpu.make_async_copy(wd_h, wd, load_sem.at[0])
    wg_copy = pltpu.make_async_copy(wg_h, wgu.at[:, 0:f], load_sem.at[1])
    wu_copy = pltpu.make_async_copy(wu_h, wgu.at[:, f : 2 * f], load_sem.at[2])
    x_copy = pltpu.make_async_copy(x_h, xv, load_sem.at[3])

    wd_copy.start()
    for c in load(0):
        c.start()
    wg_copy.start()
    wu_copy.start()
    for i in (1, 2):
        for c in load(i):
            c.start()

    barrier = pltpu.get_barrier_semaphore()
    for to in (partner, peer):
        pl.semaphore_signal(barrier, inc=1, device_id={"tp": to}, device_id_type=MESH)
    pl.semaphore_wait(barrier, 2)

    def hidden_part(i):
        for c in load(i):
            c.wait()

        @pl.when(i + 3 < steps)
        def _():
            for c in load(i + 3):
                c.start()

        b = base(i)
        other, mine_ = block(b, 1 - core), block(b, core)
        dyb = jnp.concatenate([dyv[other, :], dyv[mine_, :]], axis=0)
        for n in range(f // 256):
            cols = slice(n * 256, (n + 1) * 256)
            dh = dot_t(dyb, wd[cols, :])
            for part, r in ((dh[:R], other), (dh[R:], mine_)):
                g, u = gv[r, cols].astype(F32), uv[r, cols].astype(F32)
                sig = jax.nn.sigmoid(g)
                act = g * sig
                hid[r, cols] = (act * u).astype(BF16)
                dgu[r, cols] = ((part * u) * (sig * (1.0 + g * (1.0 - sig)))).astype(BF16)
                dgu[r, f + n * 256 : f + (n + 1) * 256] = (part * act).astype(BF16)

    def term_part(i):
        b = base(i)
        other, mine_ = block(b, 1 - core), block(b, core)
        lhs = jnp.concatenate([dgu[other, :], dgu[mine_, :]], axis=0)
        for n in range(d // 256):
            cols = slice(n * 256, (n + 1) * 256)
            t = dot_t(lhs, wgu[cols, :])
            tsend[i, :, cols] = t[:R].astype(BF16)
            own[i, :, cols] = t[R:]
        term_copy(i).start()

    def chip_sum(i):
        term_copy(i).wait_recv()
        s = own[i] + trecv[i].astype(F32)

        @pl.when(i < hs)
        def _():
            psend[i] = s.astype(BF16)
            part_copy(i).start()

        @pl.when(i >= hs)
        def _():
            own[i] = s

    wd_copy.wait()
    hidden_part(0)
    wg_copy.wait()
    wu_copy.wait()
    x_copy.start()
    term_part(0)

    @pl.loop(1, steps)
    def _(i):
        hidden_part(i)
        chip_sum(i - 1)
        term_part(i)

    chip_sum(steps - 1)

    def finish(j):
        part_copy(j).wait_recv()
        dx[mine(j), :] = (own[hs + j] + precv[j].astype(F32)).astype(BF16)
        final_copy(j).start()
        own_copy(j).start()

    def pass_on(j):
        final_copy(j).wait_recv()
        pass_copy(j).start()

    x_copy.wait()

    @pl.loop(0, d // 256)
    def _(m):
        r = pl.ds(pl.multiple_of(m * 256, 256), 256)
        xt[...] = xv[:, r].T
        for n in range(f // 256):
            cols = slice(n * 256, (n + 1) * 256)
            dwg[r, cols] = dot(xt[...], dgu[:, cols]).astype(BF16)
            dwu[r, cols] = dot(xt[...], dgu[:, f + n * 256 : f + (n + 1) * 256]).astype(BF16)
        finish(m)

    @pl.loop(0, f // 256)
    def _(m):
        r = pl.ds(pl.multiple_of(m * 256, 256), 256)
        xt[...] = hid[:, r].T
        for n in range(d // 256):
            cols = slice(n * 256, (n + 1) * 256)
            dwd[r, cols] = dot(xt[...], dyv[:, cols]).astype(BF16)
        finish(d // 256 + m)

    @pl.loop(d // 256 + f // 256, hs)
    def _(j):
        finish(j)

    @pl.loop(0, hs)
    def _(j):
        pass_on(j)

    @pl.loop(0, hs)
    def _(j):
        own_copy(j).wait_recv()
        pass_copy(j).wait_recv()
        part_copy(j).wait_send()
        final_copy(j).wait_send()
        own_copy(j).wait_send()
        pass_copy(j).wait_send()

    @pl.loop(0, steps)
    def _(i):
        term_copy(i).wait_send()


def flush(dx_v, dwg_v, dwu_v, dwd_v, dx, dwg, dwu, dwd, sem):
    copies = []
    for src, dst in ((dx_v, dx), (dwg_v, dwg), (dwu_v, dwu), (dwd_v, dwd)):
        rows = src.shape[0]
        for n in range(2):
            r = pl.ds(n * (rows // 2), rows // 2)
            copies.append(pltpu.make_async_copy(src.at[r], dst.at[r], sem.at[len(copies)]))
    for c in copies:
        c.start()
    for c in copies:
        c.wait()


def solution(mesh):
    def step(x, dy, gate, up, w_gate, w_up, w_down):
        rows, d = x.shape
        f = gate.shape[1]
        steps = rows // (2 * R)
        hs = steps // 2
        outs = [((rows, d), BF16), ((d, f), BF16), ((d, f), BF16), ((f, d), BF16)]
        dma = pltpu.SemaphoreType.DMA
        held = pl.pallas_call(
            kernel,
            out_shape=[pltpu.VMEM(s, t) for s, t in outs],
            in_specs=[pl.BlockSpec(memory_space=pl.ANY)] * 7,
            out_specs=[pl.BlockSpec(memory_space=pltpu.VMEM)] * 4,
            scratch_shapes=[
                pltpu.VMEM((rows, d), BF16),
                pltpu.VMEM((rows, d), BF16),
                pltpu.VMEM((rows, f), BF16),
                pltpu.VMEM((rows, f), BF16),
                pltpu.VMEM((d, 2 * f), BF16),
                pltpu.VMEM((f, d), BF16),
                pltpu.VMEM((rows, 2 * f), BF16),
                pltpu.VMEM((rows, f), BF16),
                pltpu.VMEM((256, rows), BF16),
                pltpu.VMEM((steps, R, d), F32),
                pltpu.VMEM((steps, R, d), BF16),
                pltpu.VMEM((steps, R, d), BF16),
                pltpu.VMEM((hs, R, d), BF16),
                pltpu.VMEM((hs, R, d), BF16),
                dma((4,)),
                dma((steps, 3)),
                dma((steps,)),
                dma((steps,)),
            ]
            + [dma((hs,))] * 8,
            compiler_params=pltpu.CompilerParams(
                collective_id=0, has_side_effects=True, vmem_limit_bytes=50 * 2**20
            ),
            name="block",
        )(x, dy, gate, up, w_gate, w_up, w_down)
        return pl.pallas_call(
            flush,
            out_shape=[jax.ShapeDtypeStruct(s, t) for s, t in outs],
            in_specs=[pl.BlockSpec(memory_space=pltpu.VMEM)] * 4,
            out_specs=[pl.BlockSpec(memory_space=pl.ANY)] * 4,
            scratch_shapes=[dma((8,))],
            compiler_params=pltpu.CompilerParams(vmem_limit_bytes=2**20),
            name="flush",
        )(*(pltpu.with_memory_space_constraint(h, pltpu.VMEM) for h in held))

    tokens, columns, rows = P("dp", None), P(None, "tp"), P("tp", None)
    return jax.shard_map(
        step,
        mesh=mesh,
        in_specs=(tokens, tokens, P("dp", "tp"), P("dp", "tp"), columns, columns, rows),
        out_specs=(tokens, P("dp", "tp"), P("dp", "tp"), P(("dp", "tp"), None)),
        check_vma=False,
    )
```

time: 122 us -> 74.1 us (0.61)
  Pallas kernels: 0 us -> 73.4 us
  waiting for transfers between devices: 57.2 us -> 0 us
  matrix products: 41.3 us -> 0 us
  between operations: 14.1 us -> 0.64 us
  local copies, waits for them, and re-layouts: 9.15 us -> 0 us
    pallas_call x0 -> x2, Pallas kernels: none -> 73.4 us  [the longest x1 69.9 us: step(): pl.pallas_call(kernel, out_shape=[pltpu.VMEM(s, t) for s, t in outs], in_...]
    psum x1 -> x0, waiting for transfers between devices: 57.2 us -> none  [step(): dx = lax.psum(term.astype(jnp.bfloat16), 'tp')]
    dot_general x6 -> x0, matrix products: 41.3 us -> none  [the longest x1 10.4 us: step(): d_hidden = jnp.dot(dy, w_down.T, preferred_element_type=jnp.float32)]
    unnamed x13 -> x0, local copies, waits for them, and re-layouts: 9.15 us -> none
  transfers between devices with their start and end apart: 1 -> 0, of which waited for: 1 -> 0; matrix products, arithmetic and copies ran while one was open for 21% -> 0% of each run, Pallas kernels for 0% -> 0%
where the time goes in v1:
time: 74.1 us; the launch traced here: 74 us
  Pallas kernels  73.4 us (99%)
    pallas_call x1, Pallas kernels, step(): pl.pallas_call(kernel, out_shape=[pltpu.VMEM(s, t) for s, t in outs], in_...  69.9 us
    pallas_call x1, Pallas kernels, step(): pl.pallas_call(flush, out_shape=[jax.ShapeDtypeStruct(s, t) for s, t in o...  3.52 us

profile of v1, /device:TPU:0, one launch (start us, length us, event | category | flops | bytes accessed | tf_op | source)
XLA Modules:
  0.0 74.0 jit_solution(9456685977484962384)
XLA Ops:
  0.6 69.9 %block.1 = (bf16[2048,1024]{1,0:T(8,128)(2,1)S(1)}, bf16[1024,768]{1,0:T(8,128)(2,1)S(1)}, bf16[1024,768]{1,0:T(8,128)(2,1)S(1)}, bf16[768,1024]{1,0:T(8,128)(2,1)S(1)}) custom-call(bf16[2048,1024]{1,0:T(8,128)(2,1)} %x_h.1, bf16[2048,1024]{1,0:T(8,128)(2,1)} %dy_h.1, bf16[2048,768]{1,0:T(8,128)(2,1)} %gate_h.1, bf16[2048,768]{1,0:T(8,128)(2,1)} %up_h.1, ...), custom_call_target="tpu_custom_call" | custom-call | tf_op jit(solution)/shard_map/block/pallas_call | solution.py:233
  70.5 3.5 %flush.1 = (bf16[2048,1024]{1,0:T(8,128)(2,1)}, bf16[1024,768]{1,0:T(8,128)(2,1)}, bf16[1024,768]{1,0:T(8,128)(2,1)}, bf16[768,1024]{1,0:T(8,128)(2,1)}) custom-call(bf16[2048,1024]{1,0:T(8,128)(2,1)S(1)} %get-tuple-element.8.dx_v, bf16[1024,768]{1,0:T(8,128)(2,1)S(1)} %get-tuple-element.9.dwg_v, bf16[1024,768]{1,0:T(8,128)(2,1)S(1)} %get-tuple-element.10.dwu_v, ...), custom_call_target="tpu_custom_call" | custom-call | tf_op jit(solution)/shard_map/flush/pallas_call | solution.py:264
